TPU v7x, 32 devices: a whole 2x2x4 slice. The times are simulated.
32 devices in a mesh: row: 4 (over x, core), col: 4 (over z), depth: 2 (over y).
Axes of the slice: x: 2, y: 2, z: 4, core: 2. Of those that a mesh axis runs over, the one named last changes fastest.
Arguments:
- trailing: float32 [3008, 48128], P('depth', ('row', 'col')), may hold values from -6 to 6
- panel_block: float32 [48128, 1024], P(('row', 'col', 'depth')), may hold values from -6 to 6
- factor_panel: float32 [48128, 1024], P(('row', 'col', 'depth')), may hold values from -0.1875 to 0.1875
- corner_block: float32 [1024, 1024], P(('row', 'col', 'depth')), may hold values from -6 to 6, as said below
- corner_inverse: float32 [1024, 1024], P(('row', 'col', 'depth')), may hold values from -1 to 2, as said below
Outputs:
- trailing_out: float32 [3008, 48128], P('depth', ('row', 'col'))
- panel_out: float32 [48128, 1024], P(('row', 'col', 'depth'))
- corner_out: float32 [1024, 1024], P(('row', 'col', 'depth'))
Inputs may be any that keep to these rules, and one draw needn't show every extreme that they name: `corner_block`: symmetric. `corner_inverse`: lower triangular, diagonal between 1 and 2.
All inputs are finite; a program needn't handle non-finite values.
Results may differ from a plain program's by a relative error of at most 0.00012.
Values sent between devices are 32-bit elements; how exact they have to be, the bound alone decides.
No kernel may reach another device: no remote copies, remote signals or barrier semaphores. Data moves between devices by JAX's collectives and lax.ppermute only.
A program may use at most 192 MiB of HBM per device.

v0:
```python
import jax
import jax.numpy as jnp
from jax import lax
from jax.sharding import PartitionSpec as P


def broadcast(value, axis, source):
    kept = jnp.where(lax.axis_index(axis) == source, value, 0).astype(value.dtype)
    return lax.psum(kept, axis)


def matmul(left, right):
    return jnp.dot(left, right, precision=lax.Precision.HIGHEST, preferred_element_type=jnp.float32)


def contract(left, right):
    return lax.dot_general(
        left,
        right,
        (((1,), (1,)), ((), ())),
        precision=lax.Precision.HIGHEST,
        preferred_element_type=jnp.float32,
    )


def body(trailing, panel_block, factor_panel, corner_block, corner_inverse):
    row_count = panel_block.shape[0]
    stacked = jnp.concatenate([panel_block, corner_block], axis=0)
    product = contract(
        stacked, lax.all_gather(corner_inverse, ("row", "col", "depth"), axis=0, tiled=True)
    )
    scaled = product[:row_count]
    right_part = product[row_count:]
    columns = corner_inverse
    corner_out = matmul(
        columns, lax.all_gather(right_part, ("row", "col", "depth"), axis=0, tiled=True)
    )
    columns = factor_panel
    coupling = matmul(
        columns, lax.all_gather(corner_out, ("row", "col", "depth"), axis=0, tiled=True)
    )
    half_panel = scaled - 0.5 * coupling
    panel_out = half_panel - 0.5 * coupling
    half_cols, lower_cols = (
        lax.all_gather(half_panel, "depth", axis=0, tiled=True),
        lax.all_gather(factor_panel, "depth", axis=0, tiled=True),
    )
    half_piece = broadcast(half_panel, ("row", "col"), 0)
    lower_piece = broadcast(factor_panel, ("row", "col"), 0)
    update = contract(half_piece, lower_cols) + contract(lower_piece, half_cols)
    trailing_out = trailing - update
    return (trailing_out, panel_out, corner_out)


def solution(mesh):
    in_specs = (
        P("depth", ("row", "col")),
        P(("row", "col", "depth"), None),
        P(("row", "col", "depth"), None),
        P(("row", "col", "depth"), None),
        P(("row", "col", "depth"), None),
    )
    out_specs = (
        P("depth", ("row", "col")),
        P(("row", "col", "depth"), None),
        P(("row", "col", "depth"), None),
    )
    return jax.shard_map(body, mesh=mesh, in_specs=in_specs, out_specs=out_specs, check_vma=False)
```

profile of v0, /device:TPU:0, one launch (start us, length us, event | category | flops | bytes accessed | tf_op | source)
XLA Modules:
  0.0 837.7 jit_solution(5062860278421330772)
XLA Ops:
  7.2 0.0 all-gather.6.cloned.1.call-start
  7.2 0.7 all-gather.6.cloned.1.call-update
  7.9 0.0 copy-start.1
  7.9 0.0 all-gather.8.cloned.1.call-start
  8.0 67.6 %all-gather.6.cloned.1.call-done = f32[1024,1024]{1,0:T(8,128)} async-done(((f32[32,1024]{1,0:T(8,128)}), f32[1024,1024]{1,0:T(8,128)}) %all-gather.6.cloned.1.call-update) | async-done | bytes 4194320 | tf_op jit(solution)/shard_map/all_gather | solution.py:30
  75.5 23.7 %fusion = f32[1536,1024]{1,0:T(8,128)S(1)} fusion(f32[1024,1024]{1,0:T(8,128)} %all-gather.6.cloned.1.call-done, f32[32,1024]{1,0:T(8,128)} %param.8, f32[1504,1024]{1,0:T(8,128)} %param.6), kind=kOutput, calls=%fused_computation.1 | convolution fusion | flops 19328925696 | bytes 16777216 | tf_op jit(solution)/shard_map/dot_general | solution.py:17
  99.2 0.0 copy-start
  99.2 2.7 copy-done
  101.9 0.7 slice.9
  102.6 0.0 all-gather.8.cloned.1.call-update
  102.6 0.0 all-gather.10.cloned.1.call-start
  102.6 60.6 %all-gather.8.cloned.1.call-done = f32[1024,1024]{1,0:T(8,128)} async-done(((f32[32,1024]{1,0:T(8,128)}), f32[1024,1024]{1,0:T(8,128)}) %all-gather.8.cloned.1.call-update) | async-done | bytes 4194320 | tf_op jit(solution)/shard_map/all_gather | solution.py:36
  163.2 0.0 copy-done.1
  163.2 5.4 convolution_bitcast_fusion
  168.6 0.0 all-gather.10.cloned.1.call-update
  168.6 0.0 all-gather.12.cloned.1.call-start
  168.7 0.5 all-gather.12.cloned.1.call-update
  169.2 0.2 all-reduce.3.cloned.1.call-start
  169.5 6.7 broadcast_select_fusion
  176.1 53.2 %all-gather.10.cloned.1.call-done = f32[1024,1024]{1,0:T(8,128)} async-done(((f32[32,1024]{1,0:T(8,128)}), f32[1024,1024]{1,0:T(8,128)}) %all-gather.10.cloned.1.call-update) | async-done | bytes 4194320 | tf_op jit(solution)/shard_map/all_gather | solution.py:40
  229.3 25.3 %bitcast_subtract_fusion = (f32[1504,1024]{1,0:T(8,128)}, f32[1504,1024]{1,0:T(8,128)}) fusion(f32[1536,1024]{1,0:T(8,128)} %copy-done, f32[1024,1024]{1,0:T(8,128)} %all-gather.10.cloned.1.call-done, f32[1504,1024]{1,0:T(8,128)} %param.7), kind=kOutput, calls=%fused_computation.6 | convolution fusion | flops 18929319936 | bytes 28835840 | tf_op jit(solution)/shard_map/dot_general | solution.py:13
  254.6 6.7 broadcast_select_fusion.1
  261.3 0.0 all-reduce.3.cloned.1.call-update
  261.4 0.0 all-gather.14.cloned.1.call-start
  261.4 0.5 all-gather.14.cloned.1.call-update
  261.9 117.2 %all-gather.12.cloned.1.call-done = f32[3008,1024]{1,0:T(8,128)} async-done(((f32[1504,1024]{1,0:T(8,128)}), f32[3008,1024]{1,0:T(8,128)}) %all-gather.12.cloned.1.call-update) | async-done | bytes 12320784 | tf_op jit(solution)/shard_map/all_gather | solution.py:46
  379.1 233.9 %all-reduce.3.cloned.1.call-done = (f32[1504,1024]{1,0:T(8,128)}, f32[1504,1024]{1,0:T(8,128)}) async-done(((f32[1504,1024]{1,0:T(8,128)}, f32[1504,1024]{1,0:T(8,128)}), (f32[1504,1024]{1,0:T(8,128)}, f32[1504,1024]{1,0:T(8,128)})) %all-reduce.3.cloned.1.call-update) | async-done | bytes 12320784 | tf_op jit(solution)/shard_map/psum | solution.py:9
  613.1 67.2 %fusion.5 = f32[1504,3008]{1,0:T(8,128)} fusion(f32[1504,1024]{1,0:T(8,128)} %get-tuple-element.3, f32[3008,1024]{1,0:T(8,128)} %all-gather.12.cloned.1.call-done), kind=kOutput, calls=%fused_computation.11 | convolution fusion | flops 55591305216 | bytes 36577280 | tf_op jit(solution)/shard_map/dot_general | solution.py:17
  680.3 83.6 %all-gather.14.cloned.1.call-done = f32[3008,1024]{1,0:T(8,128)} async-done(((f32[1504,1024]{1,0:T(8,128)}), f32[3008,1024]{1,0:T(8,128)}) %all-gather.14.cloned.1.call-update) | async-done | bytes 12320784 | tf_op jit(solution)/shard_map/all_gather | solution.py:45
  763.9 66.9 %add_subtract_fusion = f32[1504,3008]{1,0:T(8,128)} fusion(f32[1504,3008]{1,0:T(8,128)} %param.5, f32[1504,3008]{1,0:T(8,128)} %fusion.5, f32[1504,1024]{1,0:T(8,128)} %get-tuple-element.4, f32[3008,1024]{1,0:T(8,128)} %all-gather.14.cloned.1.call-done), kind=kOutput, calls=%fused_computation | convolution fusion | flops 55600353280 | bytes 72769536 | tf_op jit(solution)/shard_map/dot_general | solution.py:17
Async XLA Ops:
  7.2 68.4 %all-gather.6.cloned.1.call-start = ((), (), s32[]{:S(2)}) async-start(), calls=%async_computation | async-start | bytes 4325376 | tf_op jit(solution)/shard_map/all_gather | solution.py:30
  7.9 155.3 %copy-start.1 = (f32[32,1024]{1,0:T(8,128)S(1)}, f32[32,1024]{1,0:T(8,128)}, u32[]{:S(2)}) copy-start(f32[32,1024]{1,0:T(8,128)} %param.9) | copy-start | bytes 393220
  7.9 155.3 %all-gather.8.cloned.1.call-start = ((), (), s32[]{:S(2)}) async-start(), calls=%async_computation.1 | async-start | bytes 4325376 | tf_op jit(solution)/shard_map/all_gather | solution.py:36
  99.2 2.7 copy-start
  102.6 126.7 %all-gather.10.cloned.1.call-start = ((), (), s32[]{:S(2)}) async-start(), calls=%async_computation.2 | async-start | bytes 4325376 | tf_op jit(solution)/shard_map/all_gather | solution.py:40
  168.6 210.5 %all-gather.12.cloned.1.call-start = ((), (), s32[]{:S(2)}) async-start(), calls=%async_computation.3 | async-start | bytes 18481152 | tf_op jit(solution)/shard_map/all_gather | solution.py:46
  169.2 443.8 %all-reduce.3.cloned.1.call-start = ((), (), s32[]{:S(2)}) async-start(), calls=%async_computation.5 | async-start | bytes 24641536 | tf_op jit(solution)/shard_map/psum | solution.py:9
  261.4 502.6 %all-gather.14.cloned.1.call-start = ((), (), s32[]{:S(2)}) async-start(), calls=%async_computation.4 | async-start | bytes 18481152 | tf_op jit(solution)/shard_map/all_gather | solution.py:45
Sparse Core Ops, SparseCore 0:
  11.1 64.4 all-gather.5
  102.7 60.4 all-gather.7
  168.8 60.4 all-gather.9
  230.7 148.3 all-gather.11
  383.8 229.1 all-reduce.2
  614.5 149.4 all-gather.13
where the time goes:
time: 838 us
  waiting for transfers between devices  618 us (74%)
  matrix products  189 us (23%)
  between operations  14.1 us (2%)
  other arithmetic  13.4 us (2%)
    psum x1, waiting for transfers between devices, broadcast(): return lax.psum(kept, axis)  234 us
    dot_general x3, matrix products, contract(): lax.dot_general(left, right, (((1,), (1,)), ((), ())), precision=lax.Prec...  158 us
    all_gather x1, waiting for transfers between devices, body(): lax.all_gather(factor_panel, 'depth', axis=0, tiled=True)  117 us
    all_gather x1, waiting for transfers between devices, body(): lax.all_gather(half_panel, 'depth', axis=0, tiled=True)  83.6 us
    all_gather x1, waiting for transfers between devices, body(): lax.all_gather(corner_inverse, ('row', 'col', 'depth'), axis=0, tiled=True)  67.6 us
    all_gather x1, waiting for transfers between devices, body(): lax.all_gather(right_part, ('row', 'col', 'depth'), axis=0, tiled=True)  60.6 us
    all_gather x1, waiting for transfers between devices, body(): lax.all_gather(corner_out, ('row', 'col', 'depth'), axis=0, tiled=True)  53.2 us
    dot_general x2, matrix products, matmul(): jnp.dot(left, right, precision=lax.Precision.HIGHEST, preferred_element_t...  30.7 us
  transfers between devices with their start and end apart: 6, of which 6 were waited for; matrix products, arithmetic and copies ran while one was open for 13% of the time, Pallas kernels for 0%

commit v1 on v0

v1 whole, which is shorter than its diff:
```python
import functools

import jax
import jax.numpy as jnp
from jax import lax
from jax.experimental import pallas as pl
from jax.experimental.pallas import tpu as pltpu
from jax.sharding import PartitionSpec as P


ALL = ("row", "col", "depth")
PLANE = ("row", "col")
TILE = 256
BAND = 768
SWAP = [(0, 1), (1, 0)]
LANES = (((1,), (1,)), ((), ()))


def matmul(left, right, precision=lax.Precision.HIGH):
    return jnp.dot(left, right, precision=precision, preferred_element_type=jnp.float32)


def contract(left, right, precision=lax.Precision.HIGH):
    return lax.dot_general(
        left, right, LANES, precision=precision, preferred_element_type=jnp.float32
    )


def split(value):
    high = value.astype(jnp.bfloat16)
    return high, (value - high.astype(jnp.float32)).astype(jnp.bfloat16)


def transform(panel_rows, factor_rows, block, inverse):
    turned = matmul(factor_rows, inverse)
    return turned, contract(panel_rows - matmul(turned, block), inverse)


def corner_gather(corner_block, corner_inverse, n_depth):
    share, size = corner_block.shape
    first = lax.axis_index(ALL) * share
    row = first + lax.broadcasted_iota(jnp.int32, (share, size), 0)
    col = lax.broadcasted_iota(jnp.int32, (share, size), 1)
    square = jnp.where(col > row, corner_block, corner_inverse)
    diagonal = jnp.sum(jnp.where(col == row, corner_block, 0.0), axis=0, keepdims=True)
    mine = jnp.concatenate([square, diagonal])
    if n_depth == 2:
        other = lax.ppermute(mine, "depth", SWAP)
        lower = lax.axis_index("depth") == 0
        pair = jnp.stack([jnp.where(lower, mine, other), jnp.where(lower, other, mine)])
    else:
        pair = lax.all_gather(mine, "depth", axis=0)
    full = lax.all_gather(pair, PLANE, axis=0)
    square = full[:, :, :share].reshape(size, size)
    diagonal = jnp.sum(full[:, :, share], axis=(0, 1))
    row = lax.broadcasted_iota(jnp.int32, (size, size), 0)
    col = lax.broadcasted_iota(jnp.int32, (size, size), 1)
    block = jnp.where(col > row, square, jnp.where(col < row, square.T, diagonal[None]))
    return block, jnp.where(col > row, 0.0, square)


def slab_piece(panel_block, factor_panel, slab, n_row, n_col):
    row, col = lax.axis_index("row"), lax.axis_index("col")
    half = n_row // 2 if n_row % 2 == 0 else n_row
    groups = n_row // half
    share = -(-slab // (n_row * n_col * 8)) * 8

    def device(r, c):
        return r * n_col + c

    def take(value, r, c):
        start = min(device(r, c) * share, slab)
        stop = min(start + share, slab)
        return jnp.pad(value[start:stop], ((0, share - stop + start), (0, 0)))

    def pieces(group, place):
        return jnp.stack(
            [
                jnp.stack([take(v, group * half + k, place) for v in (panel_block, factor_panel)])
                for k in range(half)
            ]
        )

    across = {}
    for c in reversed(range(n_col)):
        across[c] = pieces(0, c)
        if groups > 1:
            sent = lax.ppermute(pieces(1, c), PLANE, [(0, device(half, 0))])
            across[c] = jnp.where(row == 0, across[c], sent)
    held = jnp.where(col == 0, across[0], 0.0)
    for c in reversed(range(1, n_col)):
        pairs = [(device(g * half, 0), device(g * half, c)) for g in range(groups)]
        held = held + lax.ppermute(across[c], PLANE, pairs)
    mine = jnp.where(row % half == 0, held[0], 0.0)
    for k in range(1, half):
        pairs = [
            (device(g * half, c), device(g * half + k, c))
            for g in range(groups)
            for c in range(n_col)
        ]
        mine = mine + lax.ppermute(held[k], PLANE, pairs)
    return mine


def update_kernel(place, slab_ref, factor_ref, panel_ref, trailing_ref, *rest):
    out_ref, left, right = rest[-3:]
    width = factor_ref.shape[1]

    @pl.when(pl.program_id(0) == 0)
    def _():
        for part in range(2):
            top, low = split(slab_ref[:, part].reshape(-1, width))
            for slot, value in enumerate((top, top, low)):
                left[:, pl.ds((2 * slot + part) * width, width)] = value

    for part, ref in enumerate((factor_ref, panel_ref)):
        top, low = split(ref[...])
        for slot, value in enumerate((top, low, top)):
            right[:, pl.ds((2 * slot + part) * width, width)] = value

    def band(index, carry):
        lines = pl.ds(pl.multiple_of(index * BAND, BAND), BAND)
        total = lax.dot_general(
            left[lines], right[...], LANES, preferred_element_type=jnp.float32
        )
        out_ref[lines] = trailing_ref[lines] - total
        return carry

    lax.fori_loop(0, left.shape[0] // BAND, band, 0)


def update(place, slab, factor_rows, panel_rows, trailing, previous):
    share = slab.shape[0] * slab.shape[2]
    width = slab.shape[3]
    rows = trailing.shape[0]
    tiles = place.shape[0]
    column_tile = pl.BlockSpec((share, TILE), lambda step, place: (0, place[step]))
    row_tile = pl.BlockSpec((TILE, width), lambda step, place: (step, 0))
    whole = pl.BlockSpec(
        slab.shape, lambda step, place: (0, 0, 0, 0), pipeline_mode=pl.Buffered(1)
    )
    operands = (place, slab, factor_rows, panel_rows, trailing)
    in_specs = [whole, row_tile, row_tile, column_tile]
    aliases = {}
    if previous is not None:
        operands += (previous,)
        in_specs.append(pl.BlockSpec(memory_space=pl.ANY))
        aliases = {5: 0}
    return pl.pallas_call(
        update_kernel,
        out_shape=jax.ShapeDtypeStruct(trailing.shape, trailing.dtype),
        grid_spec=pltpu.PrefetchScalarGridSpec(
            num_scalar_prefetch=1,
            grid=(tiles,),
            in_specs=in_specs,
            out_specs=column_tile,
            scratch_shapes=[
                pltpu.VMEM((share, 6 * width), jnp.bfloat16),
                pltpu.VMEM((TILE, 6 * width), jnp.bfloat16),
            ],
        ),
        input_output_aliases=aliases,
        compiler_params=pltpu.CompilerParams(vmem_limit_bytes=60 * 2**20),
        cost_estimate=pl.CostEstimate(
            flops=6 * tiles * TILE * rows * 2 * width,
            bytes_accessed=4 * (tiles * TILE * (2 * rows + 2 * width) + 2 * rows * width),
            transcendentals=0,
        ),
    )(*operands)


def corner_rows(corner_inverse, block, inverse):
    exact = lax.Precision.HIGHEST
    return contract(matmul(corner_inverse, block, exact), inverse, exact)


def plain(trailing, panel_block, factor_panel, corner_block, corner_inverse):
    slab = trailing.shape[0]
    sources = [lax.axis_index(a) == 0 for a in PLANE]

    def broadcast(value):
        return lax.psum(jnp.where(sources[0] & sources[1], value, 0.0), PLANE)

    block, inverse = corner_gather(corner_block, corner_inverse, 0)
    corner_out = corner_rows(corner_inverse, block, inverse)
    turned, panel_out = transform(panel_block, factor_panel, block, inverse)
    panel_cols = lax.all_gather(panel_block, "depth", axis=0, tiled=True)
    factor_cols = lax.all_gather(factor_panel, "depth", axis=0, tiled=True)
    panel_piece, turned_piece = broadcast(panel_out[:slab]), broadcast(turned[:slab])
    change = contract(panel_piece, factor_cols) + contract(turned_piece, panel_cols)
    return trailing - change, panel_out, corner_out


def paired(n_row, n_col, trailing, panel_block, factor_panel, corner_block, corner_inverse):
    slab = trailing.shape[0]
    count = panel_block.shape[0]
    lower = lax.axis_index("depth") == 0

    tiles = -(-2 * count // TILE)
    lead = -count % TILE
    full = (count - lead) // TILE - 1
    cut = lead + full * TILE
    factor_other = lax.ppermute(factor_panel, "depth", SWAP)
    panel_early = lax.ppermute(panel_block[:cut], "depth", SWAP)
    panel_late = lax.ppermute(panel_block[cut:], "depth", SWAP)

    block, inverse = corner_gather(corner_block, corner_inverse, 2)
    piece = slab_piece(panel_block, factor_panel, slab, n_row, n_col)
    piece_turned, piece_panel = transform(piece[0], piece[1], block, inverse)
    slab_rows = lax.all_gather(jnp.stack([piece_panel, piece_turned]), PLANE, axis=0)

    _, panel_out = transform(panel_block, factor_panel, block, inverse)
    corner_out = corner_rows(corner_inverse, block, inverse)

    def padded(rows, size):
        value = jnp.concatenate(rows)
        return jnp.pad(value, ((0, size - value.shape[0]), (0, 0)))

    upper = -(-count // TILE)
    first_low = (count + cut) // TILE
    first_tiles = full + tiles - upper
    assert first_low == first_tiles
    last_tiles = tiles - first_tiles

    def first_rows(own, part):
        size = first_tiles * TILE
        low = padded([own, part], size)
        high = padded([part[: full * TILE], own[lead:]], size)
        return jnp.where(lower, low, high)

    def last_rows(own, part, rest):
        size = last_tiles * TILE
        low = padded([rest], size)
        high = padded([part[full * TILE :], rest, own[:lead]], size)
        return jnp.where(lower, low, high)

    low_order = jnp.arange(tiles)
    high_order = jnp.concatenate(
        [jnp.arange(full), jnp.arange(upper, tiles), jnp.arange(full, upper)]
    )
    order = jnp.where(lower, low_order, high_order).astype(jnp.int32)
    out = update(
        order[:first_tiles],
        slab_rows,
        first_rows(factor_panel, factor_other[:cut]),
        first_rows(panel_block, panel_early),
        trailing,
        None,
    )
    out = update(
        order[first_tiles:],
        slab_rows,
        last_rows(factor_panel, factor_other[:cut], factor_other[cut:]),
        last_rows(panel_block, panel_early, panel_late),
        trailing,
        out,
    )
    return out, panel_out, corner_out


def paired_fits(n_row, n_depth, trailing, panel_block):
    count = panel_block.shape[0]
    fits = trailing.shape[1] == 2 * count and trailing.shape[0] <= count
    return n_depth == 2 and n_row % 2 == 0 and fits and count % 32 == 0 and count >= 4 * TILE


def body(n_row, n_col, n_depth, trailing, panel_block, *rest):
    if paired_fits(n_row, n_depth, trailing, panel_block):
        return paired(n_row, n_col, trailing, panel_block, *rest)
    return plain(trailing, panel_block, *rest)


def solution(mesh):
    in_specs = (P("depth", PLANE),) + (P(ALL, None),) * 4
    out_specs = (P("depth", PLANE), P(ALL, None), P(ALL, None))
    sizes = [mesh.shape[a] for a in ALL]
    return jax.shard_map(
        functools.partial(body, *sizes),
        mesh=mesh,
        in_specs=in_specs,
        out_specs=out_specs,
        check_vma=False,
    )
```

time: 838 us -> 595 us (0.71)
  waiting for transfers between devices: 618 us -> 316 us
  matrix products: 189 us -> 55.5 us
  Pallas kernels: 0 us -> 86.7 us
  other arithmetic: 13.4 us -> 53.2 us
  local copies, waits for them, and re-layouts: 3.37 us -> 34.2 us
  starting transfers between devices: 0.42 us -> 27.1 us
    all_gather x5 -> x2, waiting for transfers between devices: 382 us -> 0.02 us  [the longest x1 0.02 us: corner_gather(): full = lax.all_gather(pair, PLANE, axis=0)]
    ppermute x0 -> x12, waiting for transfers between devices: none -> 316 us  [the longest x1 214 us: paired(): panel_early = lax.ppermute(panel_block[:cut], 'depth', SWAP)]
    psum x1 -> x0, waiting for transfers between devices: 234 us -> none  [broadcast(): return lax.psum(kept, axis)]
    dot_general x5 -> x8, matrix products: 189 us -> 55.5 us  [the longest x5 36.2 us: matmul(): jnp.dot(left, right, precision=precision, preferred_element_type=jnp.floa...]
    pallas_call x0 -> x2, Pallas kernels: none -> 86.7 us  [update(): pl.pallas_call(update_kernel, out_shape=jax.ShapeDtypeStruct(trailing.sha...]
    ppermute x0 -> x12, starting transfers between devices: none -> 27.1 us  [the longest x4 12.3 us: slab_piece(): sent = lax.ppermute(pieces(1, c), PLANE, [(0, device(half, 0))])]
    select_n x2 -> x10, other arithmetic: 13.4 us -> 31.1 us  [the longest x2 17.2 us: first_rows(): return jnp.where(lower, low, high)]
    slice x1 -> x21, local copies, waits for them, and re-layouts: 0.66 us -> 15.1 us  [the longest x7 7.79 us: first_rows(): high = padded([part[:full * TILE], own[lead:]], size)]
  transfers between devices with their start and end apart: 6 -> 14, of which waited for: 6 -> 9; matrix products, arithmetic and copies ran while one was open for 13% -> 19% of each run, Pallas kernels for 0% -> 0%
where the time goes in v1:
time: 595 us; the launch traced here: 588 us
  waiting for transfers between devices  316 us (53%)
  Pallas kernels  86.7 us (15%)
  matrix products  55.5 us (9%)
  other arithmetic  53.2 us (9%)
  local copies, waits for them, and re-layouts  34.2 us (6%)
  starting transfers between devices  27.1 us (5%)
  between operations  14.7 us (2%)
    ppermute x1, waiting for transfers between devices, paired(): panel_early = lax.ppermute(panel_block[:cut], 'depth', SWAP)  214 us
    pallas_call x2, Pallas kernels, update(): pl.pallas_call(update_kernel, out_shape=jax.ShapeDtypeStruct(trailing.sha...  86.7 us
    ppermute x4, waiting for transfers between devices, slab_piece(): sent = lax.ppermute(pieces(1, c), PLANE, [(0, device(half, 0))])  55.3 us
    ppermute x1, waiting for transfers between devices, paired(): panel_late = lax.ppermute(panel_block[cut:], 'depth', SWAP)  36.6 us
    dot_general x5, matrix products, matmul(): jnp.dot(left, right, precision=precision, preferred_element_type=jnp.floa...  36.2 us
    dot_general x3, matrix products, contract(): lax.dot_general(left, right, LANES, precision=precision, preferred_elemen...  19.3 us
    select_n x2, other arithmetic, first_rows(): return jnp.where(lower, low, high)  17.2 us
    ppermute x4, starting transfers between devices, slab_piece(): sent = lax.ppermute(pieces(1, c), PLANE, [(0, device(half, 0))])  12.3 us
  transfers between devices with their start and end apart: 14, of which 9 were waited for; matrix products, arithmetic and copies ran while one was open for 19% of the time, Pallas kernels for 0%

profile of v1, /device:TPU:0, one launch (start us, length us, event | category | flops | bytes accessed | tf_op | source)
XLA Modules:
  0.0 587.5 jit_solution(10561117202382418300)
XLA Ops:
  8.3 3.1 collective-permute-start.8
  11.4 4.2 collective-permute-done.8
  16.4 4.4 slice_bitcast_fusion.32
  20.9 4.4 slice_bitcast_fusion.33
  26.6 5.0 collective-permute-start.5
  32.9 2.4 collective-permute-start.3
  36.8 2.4 collective-permute-start.1
  40.7 2.4 collective-permute-start
  47.1 6.7 %collective-permute-done.5 = f32[2,2,96,1024]{3,2,1,0:T(8,128)} collective-permute-done((f32[2,2,96,1024]{3,2,1,0:T(8,128)}, f32[2,2,96,1024]{3,2,1,0:T(8,128)}, u32[]{:S(2)}, u32[]{:S(2)}) %collective-permute-start.5) | collective-permute-done | bytes 1572896 | tf_op jit(solution)/shard_map/ppermute | solution.py:88
  53.8 1.4 maximum_select_fusion.5
  56.6 22.9 %collective-permute-done.3 = f32[2,2,96,1024]{3,2,1,0:T(8,128)} collective-permute-done((f32[2,2,96,1024]{3,2,1,0:T(8,128)}, f32[2,2,96,1024]{3,2,1,0:T(8,128)}, u32[]{:S(2)}, u32[]{:S(2)}) %collective-permute-start.3) | collective-permute-done | bytes 1572896 | tf_op jit(solution)/shard_map/ppermute | solution.py:88
  79.5 1.4 maximum_select_fusion.4
  80.9 2.5 collective-permute-start.4
  83.4 12.9 %collective-permute-done.1 = f32[2,2,96,1024]{3,2,1,0:T(8,128)} collective-permute-done((f32[2,2,96,1024]{3,2,1,0:T(8,128)}, f32[2,2,96,1024]{3,2,1,0:T(8,128)}, u32[]{:S(2)}, u32[]{:S(2)}) %collective-permute-start.1) | collective-permute-done | bytes 1572896 | tf_op jit(solution)/shard_map/ppermute | solution.py:88
  96.3 1.4 maximum_select_fusion.3
  97.7 2.4 collective-permute-start.2
  100.3 12.9 %collective-permute-done = f32[2,2,96,1024]{3,2,1,0:T(8,128)} collective-permute-done((f32[2,2,96,1024]{3,2,1,0:T(8,128)}, f32[2,2,96,1024]{3,2,1,0:T(8,128)}, u32[]{:S(2)}, u32[]{:S(2)}) %collective-permute-start) | collective-permute-done | bytes 1572896 | tf_op jit(solution)/shard_map/ppermute | solution.py:88
  113.2 4.4 collective-permute-done.2
  117.5 3.3 fusion.21
  120.9 1.5 collective-permute-start.7
  122.4 1.6 collective-permute-done.7
  125.5 6.1 %fusion.35 = (f32[16,2,32,1024]{3,2,1,0:T(8,128)}, f32[16,2,32,1024]{3,2,1,0:T(8,128)}) fusion(f32[16,2,33,1024]{3,2,1,0:T(8,128)} %bitcast.150, s32[16,2,32]{2,1,0:T(2,128)S(1)} %multiply_add_fusion), kind=kLoop, calls=%fused_computation.111 | loop fusion | flops 2097152 | bytes 12587008 | tf_op jit(solution)/shard_map/slice | solution.py:54
  131.7 5.3 copy.10
  137.0 3.7 fusion.27
  140.8 2.7 fusion.4
  143.5 1.6 fusion.36
  145.1 1.6 fusion.22
  147.7 1.7 collective-permute-start.9
  149.4 2.5 slice.203
  152.7 1.5 collective-permute-start.10
  155.2 6.4 %slice.209 = f32[1472,1024]{1,0:T(8,128)} slice(f32[1504,1024]{1,0:T(8,128)} %param.7), slice={[32:1504], [0:1024]} | slice | bytes 12058624 | tf_op jit(solution)/shard_map/slice | solution.py:228
  162.3 213.9 %collective-permute-done.11 = f32[1056,1024]{1,0:T(8,128)S(1)} collective-permute-done((f32[1056,1024]{1,0:T(8,128)S(1)}, f32[1056,1024]{1,0:T(8,128)S(1)}, u32[]{:S(2)}, u32[]{:S(2)}) %collective-permute-start.11) | collective-permute-done | bytes 4325408 | tf_op jit(solution)/shard_map/ppermute | solution.py:204
  376.3 2.2 copy-done.5
  378.4 36.6 %collective-permute-done.10 = f32[448,1024]{1,0:T(8,128)} collective-permute-done((f32[448,1024]{1,0:T(8,128)S(1)}, f32[448,1024]{1,0:T(8,128)}, u32[]{:S(2)}, u32[]{:S(2)}) %collective-permute-start.10) | collective-permute-done | bytes 1835040 | tf_op jit(solution)/shard_map/ppermute | solution.py:205
  415.1 4.1 maximum_select_fusion.1.panel_ref
  419.1 7.6 %fusion.panel_ref = f32[2560,1024]{1,0:T(8,128)} fusion(f32[1472,1024]{1,0:T(8,128)S(1)} %slice-done.4, f32[1024,1024]{1,0:T(8,128)S(1)} %slice-done.9, f32[1056,1024]{1,0:T(8,128)} %copy-done.5, f32[1504,1024]{1,0:T(8,128)S(1)} %bitcast.143, pred[]{:T(512)S(6)} %eq.21), kind=kLoop, calls=%fused_computation.1 | loop fusion | flops 15728640 | bytes 31195136 | tf_op jit(solution)/shard_map/jit(_where)/select_n | solution.py:229
  427.1 2.6 copy-done.4
  429.7 2.7 slice.221
  432.4 1.7 maximum_select_fusion.factor_ref
  434.1 1.4 slice-done.8
  435.5 9.6 %fusion.1.factor_ref = f32[2560,1024]{1,0:T(8,128)} fusion(f32[1472,1024]{1,0:T(8,128)} %slice.209, f32[1024,1024]{1,0:T(8,128)S(1)} %slice-done.8, f32[1056,1024]{1,0:T(8,128)} %slice.221, f32[1504,1024]{1,0:T(8,128)S(1)} %bitcast.145, pred[]{:T(512)S(6)} %eq.21), kind=kLoop, calls=%fused_computation.3 | loop fusion | flops 15728640 | bytes 31195136 | tf_op jit(solution)/shard_map/jit(_where)/select_n | solution.py:229
  445.1 6.7 %fusion.38 = f32[1024,32]{1,0:T(8,128)S(1)} fusion(f32[1024,1024]{1,0:T(8,128)S(1)} %copy-done.3, f32[32,1024]{1,0:T(8,128)S(1)} %copy-done.13), kind=kOutput, calls=%fused_computation.114 | convolution fusion | flops 402653184 | bytes 4456448 | tf_op jit(solution)/shard_map/dot_general | solution.py:20
  451.8 4.2 fusion.7
  456.0 12.0 %fusion.10 = f32[1024,1504]{1,0:T(8,128)S(1)} fusion(f32[1504,1024]{1,0:T(8,128)S(1)} %bitcast.145, f32[1024,1024]{1,0:T(8,128)S(1)} %bitcast.140), kind=kOutput, calls=%fused_computation.15 | convolution fusion | flops 9464446976 | bytes 16515072 | tf_op jit(solution)/shard_map/dot_general | solution.py:20
  468.0 12.2 %fusion.37 = f32[1504,1024]{1,0:T(8,128)} fusion(f32[1024,1504]{1,0:T(8,128)S(1)} %fusion.10, f32[1024,1024]{1,0:T(8,128)S(1)} %copy-done.3), kind=kOutput, calls=%fused_computation.113 | convolution fusion | flops 9462349824 | bytes 16515072 | tf_op jit(solution)/shard_map/dot_general | solution.py:20
  480.2 13.5 %fusion.2 = f32[1504,1024]{1,0:T(8,128)} fusion(f32[1504,1024]{1,0:T(8,128)S(1)} %bitcast.143, f32[1504,1024]{1,0:T(8,128)} %fusion.37, f32[1024,1024]{1,0:T(8,128)S(1)} %bitcast.141), kind=kOutput, calls=%fused_computation.5 | convolution fusion | flops 9465987072 | bytes 22675456 | tf_op jit(solution)/shard_map/dot_general | solution.py:24
  493.7 66.0 %shard_map.76.rest_0_ = f32[1504,3008]{1,0:T(8,128)} custom-call(s32[10]{0:T(128)} %bitcast.154, f32[16,2,96,1024]{3,2,1,0:T(8,128)} %bitcast.147, f32[2560,1024]{1,0:T(8,128)} %fusion.1.factor_ref, f32[2560,1024]{1,0:T(8,128)} %fusion.panel_ref, f32[1504,3008]{1,0:T(8,128)} %trailing_ref.3), custom_call_target="tpu_custom_call" | custom-call | flops 47311749120 | bytes 64094208 | tf_op jit(solution)/shard_map/pallas_call | solution.py:149
  559.8 20.7 %shard_map.77 = f32[1504,3008]{1,0:T(8,128)} custom-call(s32[2]{0:T(128)} %slice.160.place, f32[16,2,96,1024]{3,2,1,0:T(8,128)} %bitcast.148, f32[512,1024]{1,0:T(8,128)} %maximum_select_fusion.factor_ref, f32[512,1024]{1,0:T(8,128)} %maximum_select_fusion.1.panel_ref, f32[1504,3008]{1,0:T(8,128)} %trailing_ref.3, ...), custom_call_target="tpu_custom_call", output_to_operand_aliasing={{}: (5, {})} | custom-call | flops 9462349824 | bytes 22675456 | tf_op jit(solution)/shard_map/pallas_call | solution.py:149
  (95 shorter events, 18.2 us)
Async XLA Ops:
  7.2 117.1 %all-gather.5.cloned.1.call-start = ((), (), s32[]{:S(2)}) async-start(), calls=%async_computation | async-start | bytes 5570560 | tf_op jit(solution)/shard_map/all_gather | solution.py:53
  8.3 7.3 %collective-permute-start.8 = (f32[33,1024]{1,0:T(8,128)S(1)}, f32[33,1024]{1,0:T(8,128)S(1)}, u32[]{:S(2)}, u32[]{:S(2)}) collective-permute-start(f32[33,1024]{1,0:T(8,128)S(1)} %pad_maximum_fusion.6), channel_id=1, source_target_pairs={{0,1},{1,0},{2,3},{3,2},{4,5},{5,4},{6,7},{7,6},{8,9},{9,8},{10,11... | collective-permute-start | bytes 405512 | tf_op jit(solution)/shard_map/ppermute | solution.py:48
  16.4 477.4 %all-gather.7.cloned.1.call-start = ((), (), s32[]{:S(2)}) async-start(), calls=%async_computation.1 | async-start | bytes 13369344 | tf_op jit(solution)/shard_map/all_gather | solution.py:210
  26.6 8.7 %slice-start.7 = ((f32[1504,1024]{1,0:T(8,128)}), f32[64,1024]{1,0:T(8,128)S(1)}, s32[]{:S(2)}) async-start(f32[1504,1024]{1,0:T(8,128)} %param.7), calls=%async_computation.9 | async-start | bytes 524288 | tf_op jit(solution)/shard_map/slice | solution.py:74
  26.6 8.8 %slice-start.2 = ((f32[1504,1024]{1,0:T(8,128)}), f32[64,1024]{1,0:T(8,128)S(1)}, s32[]{:S(2)}) async-start(f32[1504,1024]{1,0:T(8,128)} %param.6), calls=%async_computation.4 | async-start | bytes 524288 | tf_op jit(solution)/shard_map/slice | solution.py:74
  26.6 27.2 %collective-permute-start.5 = (f32[2,2,96,1024]{3,2,1,0:T(8,128)}, f32[2,2,96,1024]{3,2,1,0:T(8,128)}, u32[]{:S(2)}, u32[]{:S(2)}) collective-permute-start(f32[2,2,96,1024]{3,2,1,0:T(8,128)} %pad_maximum_fusion.3), channel_id=1, source_target_pairs={{0,16},{1,17}} | collective-permute-start | bytes 4718600 | tf_op jit(solution)/shard_map/ppermute | solution.py:88
  32.9 46.6 %collective-permute-start.3 = (f32[2,2,96,1024]{3,2,1,0:T(8,128)}, f32[2,2,96,1024]{3,2,1,0:T(8,128)}, u32[]{:S(2)}, u32[]{:S(2)}) collective-permute-start(f32[2,2,96,1024]{3,2,1,0:T(8,128)} %pad_maximum_fusion.2), channel_id=1, source_target_pairs={{0,16},{1,17}} | collective-permute-start | bytes 4718600 | tf_op jit(solution)/shard_map/ppermute | solution.py:88
  35.5 7.6 %copy-start.11 = (f32[1,96,1024]{2,1,0:T(8,128)S(1)}, f32[1,96,1024]{2,1,0:T(8,128)}, u32[]{:S(2)}) copy-start(f32[1,96,1024]{2,1,0:T(8,128)} %get-tuple-element.21) | copy-start | bytes 1179652
  36.8 59.5 %collective-permute-start.1 = (f32[2,2,96,1024]{3,2,1,0:T(8,128)}, f32[2,2,96,1024]{3,2,1,0:T(8,128)}, u32[]{:S(2)}, u32[]{:S(2)}) collective-permute-start(f32[2,2,96,1024]{3,2,1,0:T(8,128)} %pad_maximum_fusion.1), channel_id=1, source_target_pairs={{0,16},{1,17}} | collective-permute-start | bytes 4718600 | tf_op jit(solution)/shard_map/ppermute | solution.py:88
  39.2 5.2 copy-start.9
  39.2 5.2 copy-start.10
  39.3 6.4 %copy-start.7 = (f32[1,96,1024]{2,1,0:T(8,128)S(1)}, f32[1,96,1024]{2,1,0:T(8,128)}, u32[]{:S(2)}) copy-start(f32[1,96,1024]{2,1,0:T(8,128)} %get-tuple-element.28) | copy-start | bytes 1179652
  39.4 6.4 %copy-start.8 = (f32[1,96,1024]{2,1,0:T(8,128)S(1)}, f32[1,96,1024]{2,1,0:T(8,128)}, u32[]{:S(2)}) copy-start(f32[1,96,1024]{2,1,0:T(8,128)} %get-tuple-element.29) | copy-start | bytes 1179652
  40.7 72.5 %collective-permute-start = (f32[2,2,96,1024]{3,2,1,0:T(8,128)}, f32[2,2,96,1024]{3,2,1,0:T(8,128)}, u32[]{:S(2)}, u32[]{:S(2)}) collective-permute-start(f32[2,2,96,1024]{3,2,1,0:T(8,128)} %pad_maximum_fusion), channel_id=1, source_target_pairs={{0,16},{1,17}} | collective-permute-start | bytes 4718600 | tf_op jit(solution)/shard_map/ppermute | solution.py:88
  55.2 58.0 %collective-permute-start.6 = (f32[2,2,96,1024]{3,2,1,0:T(8,128)}, f32[2,2,96,1024]{3,2,1,0:T(8,128)S(1)}, u32[]{:S(2)}, u32[]{:S(2)}) collective-permute-start(f32[2,2,96,1024]{3,2,1,0:T(8,128)} %maximum_select_fusion.5), channel_id=1, source_target_pairs={{0,2},{16,18},{1,3},{17,19}} | collective-permute-start | bytes 4718600 | tf_op jit(solution)/shard_map/ppermute | solution.py:93
  79.5 20.7 %copy-start.6 = (f32[1,96,1024]{2,1,0:T(8,128)S(1)}, f32[1,96,1024]{2,1,0:T(8,128)}, u32[]{:S(2)}) copy-start(f32[1,96,1024]{2,1,0:T(8,128)} %get-tuple-element.17) | copy-start | bytes 1179652
  80.9 32.3 %collective-permute-start.4 = (f32[2,2,96,1024]{3,2,1,0:T(8,128)}, f32[2,2,96,1024]{3,2,1,0:T(8,128)}, u32[]{:S(2)}, u32[]{:S(2)}) collective-permute-start(f32[2,2,96,1024]{3,2,1,0:T(8,128)} %maximum_select_fusion.4), channel_id=1, source_target_pairs={{0,4},{16,20},{1,5},{17,21}} | collective-permute-start | bytes 4718600 | tf_op jit(solution)/shard_map/ppermute | solution.py:93
  97.7 19.8 %collective-permute-start.2 = (f32[2,2,96,1024]{3,2,1,0:T(8,128)}, f32[2,2,96,1024]{3,2,1,0:T(8,128)}, u32[]{:S(2)}, u32[]{:S(2)}) collective-permute-start(f32[2,2,96,1024]{3,2,1,0:T(8,128)} %maximum_select_fusion.3), channel_id=1, source_target_pairs={{0,6},{16,22},{1,7},{17,23}} | collective-permute-start | bytes 4718600 | tf_op jit(solution)/shard_map/ppermute | solution.py:93
  113.2 4.4 copy-start.12
  120.9 3.2 collective-permute-start.7
  137.0 3.7 copy-start
  143.5 3.2 copy-start.2
  145.1 7.5 %slice-start = ((s8[6160384]{0:T(1024)(128)(4,1)}), s8[1966080]{0:T(1024)(128)(4,1)S(1)}, s32[]{:S(2)}) async-start(s8[6160384]{0:T(1024)(128)(4,1)} %bitcast.142), calls=%async_computation.2 | async-start | bytes 3932160
  147.7 4.9 slice-start.1
  147.7 279.1 %collective-permute-start.9 = (f32[1504,1024]{1,0:T(8,128)}, f32[1504,1024]{1,0:T(8,128)S(1)}, u32[]{:S(2)}, u32[]{:S(2)}) collective-permute-start(f32[1504,1024]{1,0:T(8,128)} %param.7), channel_id=1, source_target_pairs={{0,1},{1,0},{2,3},{3,2},{4,5},{5,4},{6,7},{7,6},{8,9},{9,8},{10,11... | collective-permute-start | bytes 18481160 | tf_op jit(solution)/shard_map/ppermute | solution.py:203
  152.0 224.2 %collective-permute-start.11 = (f32[1056,1024]{1,0:T(8,128)S(1)}, f32[1056,1024]{1,0:T(8,128)S(1)}, u32[]{:S(2)}, u32[]{:S(2)}) collective-permute-start(f32[1056,1024]{1,0:T(8,128)S(1)} %slice.203), channel_id=1, source_target_pairs={{0,1},{1,0},{2,3},{3,2},{4,5},{5,4},{6,7},{7,6},{8,9},{9,8},{10,11... | collective-permute-start | bytes 12976136 | tf_op jit(solution)/shard_map/ppermute | solution.py:204
  152.7 262.3 %collective-permute-start.10 = (f32[448,1024]{1,0:T(8,128)S(1)}, f32[448,1024]{1,0:T(8,128)}, u32[]{:S(2)}, u32[]{:S(2)}) collective-permute-start(f32[448,1024]{1,0:T(8,128)S(1)} %slice.202), channel_id=1, source_target_pairs={{0,1},{1,0},{2,3},{3,2},{4,5},{5,4},{6,7},{7,6},{8,9},{9,8},{10,11... | collective-permute-start | bytes 5505032 | tf_op jit(solution)/shard_map/ppermute | solution.py:205
  161.7 214.6 %copy-start.14 = (s32[12]{0:T(128)}, s32[12]{0:T(128)S(1)}, u32[]{:S(2)}) copy-start(s32[12]{0:T(128)S(1)} %broadcast_select_fusion) | copy-start | bytes 148
  376.2 2.2 copy-start.5
  376.2 38.8 %slice-start.3 = ((f32[1504,1024]{1,0:T(8,128)}), f32[32,1024]{1,0:T(8,128)S(1)}, s32[]{:S(2)}) async-start(f32[1504,1024]{1,0:T(8,128)} %param.6), calls=%async_computation.5 | async-start | bytes 262144 | tf_op jit(solution)/shard_map/slice | solution.py:234
  376.2 42.9 %slice-start.4 = ((f32[1504,1024]{1,0:T(8,128)}), f32[1472,1024]{1,0:T(8,128)S(1)}, s32[]{:S(2)}) async-start(f32[1504,1024]{1,0:T(8,128)} %param.6), calls=%async_computation.6 | async-start | bytes 12058624 | tf_op jit(solution)/shard_map/slice | solution.py:228
  415.1 4.1 slice-start.9
  426.7 3.0 copy-start.4
  427.1 7.0 %slice-start.5 = ((s8[6160384]{0:T(1024)(128)(4,1)}), s8[4194304]{0:T(1024)(128)(4,1)S(1)}, s32[]{:S(2)}) async-start(s8[6160384]{0:T(1024)(128)(4,1)} %bitcast.144), calls=%async_computation.7 | async-start | bytes 8388608
  429.7 4.4 slice-start.6
  432.4 3.1 slice-start.8
  435.5 9.6 %copy-start.3 = (f32[1024,1024]{1,0:T(8,128)S(1)}, f32[1024,1024]{1,0:T(8,128)}, u32[]{:S(2)}) copy-start(f32[1024,1024]{1,0:T(8,128)} %copy-done.2) | copy-start | bytes 12582916
  435.5 9.6 %copy-start.13 = (f32[32,1024]{1,0:T(8,128)S(1)}, f32[32,1024]{1,0:T(8,128)}, u32[]{:S(2)}) copy-start(f32[32,1024]{1,0:T(8,128)} %param.9) | copy-start | bytes 393220
  445.1 6.7 %copy-start.1 = (f32[16,2,32,1024]{3,2,1,0:T(8,128)S(1)}, f32[16,2,32,1024]{3,2,1,0:T(8,128)}, u32[]{:S(2)}) copy-start(f32[16,2,32,1024]{3,2,1,0:T(8,128)} %get-tuple-element.33) | copy-start | bytes 12582916
Sparse Core Ops, SparseCore 0:
  16.5 57.1 all-gather.4
  147.8 105.0 all-gather.6

commit v2 on v1

--- a/solution.py
+++ b/solution.py
@@ -1,4 +1,5 @@
 import functools
+import math
 
 import jax
 import jax.numpy as jnp
@@ -34,6 +35,15 @@
 def transform(panel_rows, factor_rows, block, inverse):
     turned = matmul(factor_rows, inverse)
     return turned, contract(panel_rows - matmul(turned, block), inverse)
+
+
+def transform_with_corner(panel_rows, factor_rows, corner_inverse, block, inverse):
+    count = panel_rows.shape[0]
+    turned = matmul(factor_rows, inverse)
+    middle = matmul(jnp.concatenate([turned, corner_inverse]), block)
+    rest = jnp.concatenate([panel_rows - middle[:count], middle[count:]])
+    result = contract(rest, inverse)
+    return turned, result[:count], result[count:]
 
 
 def corner_gather(corner_block, corner_inverse, n_depth):
@@ -61,45 +71,48 @@
 
 def slab_piece(panel_block, factor_panel, slab, n_row, n_col):
     row, col = lax.axis_index("row"), lax.axis_index("col")
-    half = n_row // 2 if n_row % 2 == 0 else n_row
-    groups = n_row // half
+    half = n_row // 2
+    groups = 2
     share = -(-slab // (n_row * n_col * 8)) * 8
 
     def device(r, c):
         return r * n_col + c
 
-    def take(value, r, c):
-        start = min(device(r, c) * share, slab)
-        stop = min(start + share, slab)
-        return jnp.pad(value[start:stop], ((0, share - stop + start), (0, 0)))
-
     def pieces(group, place):
-        return jnp.stack(
-            [
-                jnp.stack([take(v, group * half + k, place) for v in (panel_block, factor_panel)])
-                for k in range(half)
-            ]
-        )
+        start = min((group * n_col + place) * half * share, slab)
+        stop = min(start + half * share, slab)
+        rows = ((0, half * share - stop + start), (0, 0))
+        return jnp.stack([jnp.pad(v[start:stop], rows) for v in (panel_block, factor_panel)])
 
     across = {}
     for c in reversed(range(n_col)):
-        across[c] = pieces(0, c)
-        if groups > 1:
-            sent = lax.ppermute(pieces(1, c), PLANE, [(0, device(half, 0))])
-            across[c] = jnp.where(row == 0, across[c], sent)
+        sent = lax.ppermute(pieces(1, c), PLANE, [(0, device(half, 0))])
+        across[c] = jnp.where(row == 0, pieces(0, c), sent)
     held = jnp.where(col == 0, across[0], 0.0)
     for c in reversed(range(1, n_col)):
         pairs = [(device(g * half, 0), device(g * half, c)) for g in range(groups)]
         held = held + lax.ppermute(across[c], PLANE, pairs)
-    mine = jnp.where(row % half == 0, held[0], 0.0)
+    mine = jnp.where(row % half == 0, held[:, :share], 0.0)
     for k in range(1, half):
         pairs = [
             (device(g * half, c), device(g * half + k, c))
             for g in range(groups)
             for c in range(n_col)
         ]
-        mine = mine + lax.ppermute(held[k], PLANE, pairs)
+        mine = mine + lax.ppermute(held[:, k * share : (k + 1) * share], PLANE, pairs)
     return mine
+
+
+def lay_slab(slab_ref, left):
+    groups, half, columns, parts, share, width = slab_ref.shape
+    for g in range(groups):
+        for k in range(half):
+            for c in range(columns):
+                lines = pl.ds(((g * columns + c) * half + k) * share, share)
+                for part in range(parts):
+                    top, low = split(slab_ref[g, k, c, part])
+                    for slot, value in enumerate((top, top, low)):
+                        left[lines, pl.ds((2 * slot + part) * width, width)] = value
 
 
 def update_kernel(place, slab_ref, factor_ref, panel_ref, trailing_ref, *rest):
@@ -108,10 +121,7 @@
 
     @pl.when(pl.program_id(0) == 0)
     def _():
-        for part in range(2):
-            top, low = split(slab_ref[:, part].reshape(-1, width))
-            for slot, value in enumerate((top, top, low)):
-                left[:, pl.ds((2 * slot + part) * width, width)] = value
+        lay_slab(slab_ref, left)
 
     for part, ref in enumerate((factor_ref, panel_ref)):
         top, low = split(ref[...])
@@ -130,14 +140,14 @@
 
 
 def update(place, slab, factor_rows, panel_rows, trailing, previous):
-    share = slab.shape[0] * slab.shape[2]
-    width = slab.shape[3]
+    share = math.prod(slab.shape[:3]) * slab.shape[4]
+    width = slab.shape[5]
     rows = trailing.shape[0]
     tiles = place.shape[0]
     column_tile = pl.BlockSpec((share, TILE), lambda step, place: (0, place[step]))
     row_tile = pl.BlockSpec((TILE, width), lambda step, place: (step, 0))
     whole = pl.BlockSpec(
-        slab.shape, lambda step, place: (0, 0, 0, 0), pipeline_mode=pl.Buffered(1)
+        slab.shape, lambda step, place: (0,) * 6, pipeline_mode=pl.Buffered(1)
     )
     operands = (place, slab, factor_rows, panel_rows, trailing)
     in_specs = [whole, row_tile, row_tile, column_tile]
@@ -169,6 +179,62 @@
     )(*operands)
 
 
+def bands_kernel(place, slab_ref, factor_ref, panel_ref, trailing_ref, _, out_ref, left, right):
+    width = factor_ref.shape[1]
+
+    @pl.when(pl.program_id(0) == 0)
+    def _():
+        for part, ref in enumerate((factor_ref, panel_ref)):
+            top, low = split(ref[...])
+            for slot, value in enumerate((top, low, top)):
+                right[:, pl.ds((2 * slot + part) * width, width)] = value
+
+    lay_slab(slab_ref, left)
+    total = lax.dot_general(left[...], right[...], LANES, preferred_element_type=jnp.float32)
+    out_ref[...] = trailing_ref[...] - total
+
+
+def update_bands(place, slab, factor_rows, panel_rows, trailing, previous):
+    groups, half, places, _, share, width = slab.shape
+    pack = 2 if places % 2 == 0 else 1
+    across = places // pack
+    lines = half * pack * share
+    columns = factor_rows.shape[0]
+    rows = trailing.shape[0]
+    tile = pl.BlockSpec((lines, columns), lambda step, place: (step, place[0]))
+    fixed = pl.BlockSpec((columns, width), lambda step, place: (0, 0), pipeline_mode=pl.Buffered(1))
+    return pl.pallas_call(
+        bands_kernel,
+        out_shape=jax.ShapeDtypeStruct(trailing.shape, trailing.dtype),
+        grid_spec=pltpu.PrefetchScalarGridSpec(
+            num_scalar_prefetch=1,
+            grid=(groups * across,),
+            in_specs=[
+                pl.BlockSpec(
+                    (1, half, pack, 2, share, width),
+                    lambda step, place: (step // across, 0, step % across, 0, 0, 0),
+                ),
+                fixed,
+                fixed,
+                tile,
+                pl.BlockSpec(memory_space=pl.ANY),
+            ],
+            out_specs=tile,
+            scratch_shapes=[
+                pltpu.VMEM((lines, 6 * width), jnp.bfloat16),
+                pltpu.VMEM((columns, 6 * width), jnp.bfloat16),
+            ],
+        ),
+        input_output_aliases={5: 0},
+        compiler_params=pltpu.CompilerParams(vmem_limit_bytes=48 * 2**20),
+        cost_estimate=pl.CostEstimate(
+            flops=6 * columns * rows * 2 * width,
+            bytes_accessed=4 * (columns * (2 * rows + 2 * width) + 2 * rows * width),
+            transcendentals=0,
+        ),
+    )(place, slab, factor_rows, panel_rows, trailing, previous)
+
+
 def corner_rows(corner_inverse, block, inverse):
     exact = lax.Precision.HIGHEST
     return contract(matmul(corner_inverse, block, exact), inverse, exact)
@@ -200,17 +266,20 @@
     lead = -count % TILE
     full = (count - lead) // TILE - 1
     cut = lead + full * TILE
-    factor_other = lax.ppermute(factor_panel, "depth", SWAP)
-    panel_early = lax.ppermute(panel_block[:cut], "depth", SWAP)
-    panel_late = lax.ppermute(panel_block[cut:], "depth", SWAP)
+    early, late = {}, {}
+    for name, value in (("factor", factor_panel), ("panel", panel_block)):
+        early[name] = lax.ppermute(value[:cut], "depth", SWAP)
+        late[name] = lax.ppermute(value[cut:], "depth", SWAP)
 
     block, inverse = corner_gather(corner_block, corner_inverse, 2)
     piece = slab_piece(panel_block, factor_panel, slab, n_row, n_col)
-    piece_turned, piece_panel = transform(piece[0], piece[1], block, inverse)
+    piece_turned, piece_panel, corner_out = transform_with_corner(
+        piece[0], piece[1], corner_inverse, block, inverse
+    )
     slab_rows = lax.all_gather(jnp.stack([piece_panel, piece_turned]), PLANE, axis=0)
+    slab_rows = slab_rows.reshape(2, n_row // 2, n_col, *slab_rows.shape[1:])
 
     _, panel_out = transform(panel_block, factor_panel, block, inverse)
-    corner_out = corner_rows(corner_inverse, block, inverse)
 
     def padded(rows, size):
         value = jnp.concatenate(rows)
@@ -239,22 +308,16 @@
         [jnp.arange(full), jnp.arange(upper, tiles), jnp.arange(full, upper)]
     )
     order = jnp.where(lower, low_order, high_order).astype(jnp.int32)
-    out = update(
-        order[:first_tiles],
-        slab_rows,
-        first_rows(factor_panel, factor_other[:cut]),
-        first_rows(panel_block, panel_early),
-        trailing,
-        None,
-    )
-    out = update(
-        order[first_tiles:],
-        slab_rows,
-        last_rows(factor_panel, factor_other[:cut], factor_other[cut:]),
-        last_rows(panel_block, panel_early, panel_late),
-        trailing,
-        out,
-    )
+    factor_rows = first_rows(factor_panel, early["factor"])
+    panel_rows = first_rows(panel_block, early["panel"])
+    out = update(order[:first_tiles], slab_rows, factor_rows, panel_rows, trailing, None)
+    factor_rows = last_rows(factor_panel, early["factor"], late["factor"])
+    panel_rows = last_rows(panel_block, early["panel"], late["panel"])
+    place = order[first_tiles:]
+    if full % last_tiles == 0 and first_low % last_tiles == 0 and upper - full == last_tiles:
+        out = update_bands(place[:1] // last_tiles, slab_rows, factor_rows, panel_rows, trailing, out)
+    else:
+        out = update(place, slab_rows, factor_rows, panel_rows, trailing, out)
     return out, panel_out, corner_out
 
 

time: 595 us -> 580 us (0.975)
    pallas_call x2 -> x1, Pallas kernels: 86.7 us -> 66.2 us  [update(): pl.pallas_call(update_kernel, out_shape=jax.ShapeDtypeStruct(trailing.sha...]
    pallas_call x0 -> x1, Pallas kernels: none -> 14.5 us  [update_bands(): pl.pallas_call(bands_kernel, out_shape=jax.ShapeDtypeStruct(trailing.shap...]
    ppermute x4 -> x5, waiting for transfers between devices: 252 us -> 246 us  [the longest x2 172 us: paired(): early[name] = lax.ppermute(value[:cut], 'depth', SWAP)]
    dot_general x3 -> x2, matrix products: 19.3 us -> 15.5 us  [contract(): lax.dot_general(left, right, LANES, precision=precision, preferred_elemen...]
    dot_general x5 -> x4, matrix products: 36.2 us -> 35.9 us  [matmul(): jnp.dot(left, right, precision=precision, preferred_element_type=jnp.floa...]
  transfers between devices with their start and end apart: 14 -> 15, of which waited for: 9 -> 11; matrix products, arithmetic and copies ran while one was open for 19% -> 18% of each run, Pallas kernels for 0% -> 0%
where the time goes in v2:
time: 580 us; the launch traced here: 575 us
  waiting for transfers between devices  314 us (54%)
  Pallas kernels  80.8 us (14%)
  matrix products  51.4 us (9%)
  other arithmetic  48.7 us (8%)
  local copies, waits for them, and re-layouts  35.1 us (6%)
  starting transfers between devices  28 us (5%)
  between operations  17.2 us (3%)
    ppermute x2, waiting for transfers between devices, paired(): early[name] = lax.ppermute(value[:cut], 'depth', SWAP)  172 us
    ppermute x2, waiting for transfers between devices, paired(): late[name] = lax.ppermute(value[cut:], 'depth', SWAP)  72.1 us
    pallas_call x1, Pallas kernels, update(): pl.pallas_call(update_kernel, out_shape=jax.ShapeDtypeStruct(trailing.sha...  66.2 us
    ppermute x4, waiting for transfers between devices, slab_piece(): sent = lax.ppermute(pieces(1, c), PLANE, [(0, device(half, 0))])  58 us
    dot_general x4, matrix products, matmul(): jnp.dot(left, right, precision=precision, preferred_element_type=jnp.floa...  35.9 us
    select_n x2, other arithmetic, first_rows(): return jnp.where(lower, low, high)  17.4 us
    dot_general x2, matrix products, contract(): lax.dot_general(left, right, LANES, precision=precision, preferred_elemen...  15.5 us
    pallas_call x1, Pallas kernels, update_bands(): pl.pallas_call(bands_kernel, out_shape=jax.ShapeDtypeStruct(trailing.shap...  14.5 us
  transfers between devices with their start and end apart: 15, of which 11 were waited for; matrix products, arithmetic and copies ran while one was open for 18% of the time, Pallas kernels for 0%

profile of v2, /device:TPU:0, one launch (start us, length us, event | category | flops | bytes accessed | tf_op | source)
XLA Modules:
  0.0 574.8 jit_solution(11059438343099913881)
XLA Ops:
  8.3 3.1 collective-permute-start.8
  11.4 4.2 collective-permute-done.8
  16.4 4.4 slice_bitcast_fusion.13
  20.8 4.4 slice_bitcast_fusion.12
  26.4 5.0 collective-permute-start.3
  31.4 1.3 pad_maximum_fusion.3
  32.7 2.4 collective-permute-start.5
  36.7 2.5 collective-permute-start.1
  40.4 2.4 collective-permute-start
  42.9 10.5 %collective-permute-done.3 = f32[2,192,1024]{2,1,0:T(8,128)} collective-permute-done((f32[2,192,1024]{2,1,0:T(8,128)}, f32[2,192,1024]{2,1,0:T(8,128)}, u32[]{:S(2)}, u32[]{:S(2)}) %collective-permute-start.3) | collective-permute-done | bytes 1572896 | tf_op jit(solution)/shard_map/ppermute | solution.py:89
  53.4 1.4 maximum_select_fusion.4
  54.8 2.5 collective-permute-start.4
  57.3 22.0 %collective-permute-done.5 = f32[2,192,1024]{2,1,0:T(8,128)} collective-permute-done((f32[2,192,1024]{2,1,0:T(8,128)}, f32[2,192,1024]{2,1,0:T(8,128)}, u32[]{:S(2)}, u32[]{:S(2)}) %collective-permute-start.5) | collective-permute-done | bytes 1572896 | tf_op jit(solution)/shard_map/ppermute | solution.py:89
  79.3 3.0 maximum_select_fusion.5
  82.3 2.4 collective-permute-start.6
  84.7 11.4 %collective-permute-done.1 = f32[2,192,1024]{2,1,0:T(8,128)} collective-permute-done((f32[2,192,1024]{2,1,0:T(8,128)}, f32[2,192,1024]{2,1,0:T(8,128)}, u32[]{:S(2)}, u32[]{:S(2)}) %collective-permute-start.1) | collective-permute-done | bytes 1572896 | tf_op jit(solution)/shard_map/ppermute | solution.py:89
  96.2 1.5 maximum_select_fusion.3
  97.6 1.4 collective-permute-start.2
  99.0 14.0 %collective-permute-done = f32[2,192,1024]{2,1,0:T(8,128)} collective-permute-done((f32[2,192,1024]{2,1,0:T(8,128)}, f32[2,192,1024]{2,1,0:T(8,128)}, u32[]{:S(2)}, u32[]{:S(2)}) %collective-permute-start) | collective-permute-done | bytes 1572896 | tf_op jit(solution)/shard_map/ppermute | solution.py:89
  113.0 5.7 collective-permute-done.2
  119.8 3.3 fusion.18
  123.2 1.6 collective-permute-start.7
  124.8 1.5 collective-permute-done.7
  127.8 6.1 %fusion.37 = (f32[16,2,32,1024]{3,2,1,0:T(8,128)}, f32[16,2,32,1024]{3,2,1,0:T(8,128)}) fusion(f32[16,2,33,1024]{3,2,1,0:T(8,128)} %bitcast.79, s32[16,2,32]{2,1,0:T(2,128)S(1)} %multiply_add_fusion), kind=kLoop, calls=%fused_computation.84 | loop fusion | flops 2097152 | bytes 12587008 | tf_op jit(solution)/shard_map/slice | solution.py:64
  134.0 5.3 copy.10
  139.3 3.7 fusion.30
  143.1 3.8 fusion.21
  146.9 1.6 fusion.10
  149.6 2.9 slice.149
  152.6 1.6 collective-permute-start.10
  154.2 5.2 slice.153
  160.4 1.4 slice.148
  167.3 81.6 %collective-permute-done.10 = f32[1056,1024]{1,0:T(8,128)S(1)} collective-permute-done((f32[1056,1024]{1,0:T(8,128)S(1)}, f32[1056,1024]{1,0:T(8,128)S(1)}, u32[]{:S(2)}, u32[]{:S(2)}) %collective-permute-start.10) | collective-permute-done | bytes 4325408 | tf_op jit(solution)/shard_map/ppermute | solution.py:271
  248.9 2.2 copy-done.3
  251.1 90.5 %collective-permute-done.12 = f32[1056,1024]{1,0:T(8,128)S(1)} collective-permute-done((f32[1056,1024]{1,0:T(8,128)}, f32[1056,1024]{1,0:T(8,128)S(1)}, u32[]{:S(2)}, u32[]{:S(2)}) %collective-permute-start.12) | collective-permute-done | bytes 4325408 | tf_op jit(solution)/shard_map/ppermute | solution.py:271
  341.6 2.6 slice.174
  345.2 35.8 %collective-permute-done.9 = f32[448,1024]{1,0:T(8,128)} collective-permute-done((f32[448,1024]{1,0:T(8,128)}, f32[448,1024]{1,0:T(8,128)}, u32[]{:S(2)}, u32[]{:S(2)}) %collective-permute-start.9) | collective-permute-done | bytes 1835040 | tf_op jit(solution)/shard_map/ppermute | solution.py:272
  381.0 2.5 maximum_select_fusion.factor_ref
  383.5 36.3 %collective-permute-done.11 = f32[448,1024]{1,0:T(8,128)} collective-permute-done((f32[448,1024]{1,0:T(8,128)S(1)}, f32[448,1024]{1,0:T(8,128)}, u32[]{:S(2)}, u32[]{:S(2)}) %collective-permute-start.11) | collective-permute-done | bytes 1835040 | tf_op jit(solution)/shard_map/ppermute | solution.py:272
  419.8 4.1 maximum_select_fusion.1.panel_ref
  423.9 9.7 %fusion.panel_ref = f32[2560,1024]{1,0:T(8,128)} fusion(f32[1472,1024]{1,0:T(8,128)S(1)} %slice-done.13, f32[1024,1024]{1,0:T(8,128)} %slice.174, f32[1056,1024]{1,0:T(8,128)} %copy-done.4, f32[1504,1024]{1,0:T(8,128)S(1)} %bitcast.68, pred[]{:T(512)S(6)} %eq.21), kind=kLoop, calls=%fused_computation.1 | loop fusion | flops 15728640 | bytes 31195136 | tf_op jit(solution)/shard_map/jit(_where)/select_n | solution.py:298
  434.8 7.7 %fusion.1.factor_ref = f32[2560,1024]{1,0:T(8,128)} fusion(f32[1472,1024]{1,0:T(8,128)S(1)} %slice-done.6, f32[1024,1024]{1,0:T(8,128)S(1)} %slice-done.15, f32[1056,1024]{1,0:T(8,128)} %copy-done.3, f32[1504,1024]{1,0:T(8,128)S(1)} %bitcast.64, pred[]{:T(512)S(6)} %eq.21), kind=kLoop, calls=%fused_computation.3 | loop fusion | flops 15728640 | bytes 31195136 | tf_op jit(solution)/shard_map/jit(_where)/select_n | solution.py:298
  443.1 14.2 %fusion.8 = f32[1024,1504]{1,0:T(8,128)} fusion(f32[1504,1024]{1,0:T(8,128)S(1)} %bitcast.64, f32[1024,1024]{1,0:T(8,128)S(1)} %bitcast.72), kind=kOutput, calls=%fused_computation.14 | convolution fusion | flops 9464446976 | bytes 16515072 | tf_op jit(solution)/shard_map/dot_general | solution.py:21
  457.3 14.3 %fusion.19 = f32[1504,1024]{1,0:T(8,128)} fusion(f32[1024,1504]{1,0:T(8,128)} %fusion.8, f32[1024,1024]{1,0:T(8,128)S(1)} %bitcast.73, f32[1024,1024]{0,1:T(8,128)S(1)} %copy-done.5, f32[1024]{0:T(1024)S(1)} %slice_reduce_fusion), kind=kOutput, calls=%fused_computation.33 | convolution fusion | flops 9466544128 | bytes 20713472 | tf_op jit(solution)/shard_map/dot_general | solution.py:21
  471.5 13.8 %fusion.2 = f32[1504,1024]{1,0:T(8,128)} fusion(f32[1504,1024]{1,0:T(8,128)S(1)} %bitcast.68, f32[1504,1024]{1,0:T(8,128)} %fusion.19, f32[1024,1024]{1,0:T(8,128)S(1)} %bitcast.74), kind=kOutput, calls=%fused_computation.5 | convolution fusion | flops 9465987072 | bytes 22675456 | tf_op jit(solution)/shard_map/dot_general | solution.py:25
  485.4 66.2 %shard_map.76._ = f32[1504,3008]{1,0:T(8,128)} custom-call(s32[10]{0:T(128)} %bitcast.83, f32[2,2,4,2,96,1024]{5,4,3,2,1,0:T(8,128)} %bitcast.76, f32[2560,1024]{1,0:T(8,128)} %fusion.1.factor_ref, f32[2560,1024]{1,0:T(8,128)} %fusion.panel_ref, f32[1504,3008]{1,0:T(8,128)} %trailing_ref.3), custom_call_target="tpu_custom_call" | custom-call | flops 47311749120 | bytes 64094208 | tf_op jit(solution)/shard_map/pallas_call | solution.py:159
  551.6 1.6 copy-done
  553.2 14.5 %shard_map.77 = f32[1504,3008]{1,0:T(8,128)} custom-call(s32[1]{0:T(128)S(6)} %select_n.119.place, f32[2,2,4,2,96,1024]{5,4,3,2,1,0:T(8,128)} %bitcast.77, f32[512,1024]{1,0:T(8,128)S(1)} %maximum_select_fusion.factor_ref, f32[512,1024]{1,0:T(8,128)S(1)} %copy-done, f32[1504,3008]{1,0:T(8,128)} %trailing_ref.3, ...), custom_call_target="tpu_custom_call", output_to_operand_aliasing={{}: (5, {})} | custom-call | flops 9462349824 | bytes 22675456 | tf_op jit(solution)/shard_map/pallas_call | solution.py:206
  (97 shorter events, 16.5 us)
Async XLA Ops:
  7.2 119.4 %all-gather.5.cloned.1.call-start = ((), (), s32[]{:S(2)}) async-start(), calls=%async_computation | async-start | bytes 5570560 | tf_op jit(solution)/shard_map/all_gather | solution.py:63
  8.3 7.3 %collective-permute-start.8 = (f32[33,1024]{1,0:T(8,128)S(1)}, f32[33,1024]{1,0:T(8,128)S(1)}, u32[]{:S(2)}, u32[]{:S(2)}) collective-permute-start(f32[33,1024]{1,0:T(8,128)S(1)} %pad_maximum_fusion.6), channel_id=1, source_target_pairs={{0,1},{1,0},{2,3},{3,2},{4,5},{5,4},{6,7},{7,6},{8,9},{9,8},{10,11... | collective-permute-start | bytes 405512 | tf_op jit(solution)/shard_map/ppermute | solution.py:58
  16.4 469.0 %all-gather.7.cloned.1.call-start = ((), (), s32[]{:S(2)}) async-start(), calls=%async_computation.1 | async-start | bytes 13369344 | tf_op jit(solution)/shard_map/all_gather | solution.py:279
  25.2 10.0 %slice-start.11 = ((f32[1504,1024]{1,0:T(8,128)}), f32[160,1024]{1,0:T(8,128)S(1)}, s32[]{:S(2)}) async-start(f32[1504,1024]{1,0:T(8,128)} %param.6), calls=%async_computation.13 | async-start | bytes 1310720 | tf_op jit(solution)/shard_map/slice | solution.py:85
  26.4 8.8 %slice-start.4 = ((f32[1504,1024]{1,0:T(8,128)}), f32[160,1024]{1,0:T(8,128)S(1)}, s32[]{:S(2)}) async-start(f32[1504,1024]{1,0:T(8,128)} %param.7), calls=%async_computation.6 | async-start | bytes 1310720 | tf_op jit(solution)/shard_map/slice | solution.py:85
  26.4 26.9 %collective-permute-start.3 = (f32[2,192,1024]{2,1,0:T(8,128)}, f32[2,192,1024]{2,1,0:T(8,128)}, u32[]{:S(2)}, u32[]{:S(2)}) collective-permute-start(f32[2,192,1024]{2,1,0:T(8,128)} %pad_maximum_fusion.2), channel_id=1, source_target_pairs={{0,16},{1,17}} | collective-permute-start | bytes 4718600 | tf_op jit(solution)/shard_map/ppermute | solution.py:89
  32.7 46.6 %collective-permute-start.5 = (f32[2,192,1024]{2,1,0:T(8,128)}, f32[2,192,1024]{2,1,0:T(8,128)}, u32[]{:S(2)}, u32[]{:S(2)}) collective-permute-start(f32[2,192,1024]{2,1,0:T(8,128)} %pad_maximum_fusion.3), channel_id=1, source_target_pairs={{0,16},{1,17}} | collective-permute-start | bytes 4718600 | tf_op jit(solution)/shard_map/ppermute | solution.py:89
  35.3 18.1 %copy-start.8 = (f32[1,192,1024]{2,1,0:T(8,128)S(1)}, f32[1,192,1024]{2,1,0:T(8,128)}, u32[]{:S(2)}) copy-start(f32[1,192,1024]{2,1,0:T(8,128)} %get-tuple-element.7) | copy-start | bytes 2359300
  35.3 18.0 %copy-start.9 = (f32[1,192,1024]{2,1,0:T(8,128)S(1)}, f32[1,192,1024]{2,1,0:T(8,128)}, u32[]{:S(2)}) copy-start(f32[1,192,1024]{2,1,0:T(8,128)} %get-tuple-element.14) | copy-start | bytes 2359300
  36.7 59.5 %collective-permute-start.1 = (f32[2,192,1024]{2,1,0:T(8,128)}, f32[2,192,1024]{2,1,0:T(8,128)}, u32[]{:S(2)}, u32[]{:S(2)}) collective-permute-start(f32[2,192,1024]{2,1,0:T(8,128)} %pad_maximum_fusion.1), channel_id=1, source_target_pairs={{0,16},{1,17}} | collective-permute-start | bytes 4718600 | tf_op jit(solution)/shard_map/ppermute | solution.py:89
  40.4 72.6 %collective-permute-start = (f32[2,192,1024]{2,1,0:T(8,128)}, f32[2,192,1024]{2,1,0:T(8,128)}, u32[]{:S(2)}, u32[]{:S(2)}) collective-permute-start(f32[2,192,1024]{2,1,0:T(8,128)} %pad_maximum_fusion), channel_id=1, source_target_pairs={{0,16},{1,17}} | collective-permute-start | bytes 4718600 | tf_op jit(solution)/shard_map/ppermute | solution.py:89
  54.8 58.3 %collective-permute-start.4 = (f32[2,192,1024]{2,1,0:T(8,128)}, f32[2,192,1024]{2,1,0:T(8,128)}, u32[]{:S(2)}, u32[]{:S(2)}) collective-permute-start(f32[2,192,1024]{2,1,0:T(8,128)} %maximum_select_fusion.4), channel_id=1, source_target_pairs={{0,4},{16,20},{1,5},{17,21}} | collective-permute-start | bytes 4718600 | tf_op jit(solution)/shard_map/ppermute | solution.py:94
  79.3 40.5 %copy-start.6 = (f32[1,192,1024]{2,1,0:T(8,128)S(1)}, f32[1,192,1024]{2,1,0:T(8,128)}, u32[]{:S(2)}) copy-start(f32[1,192,1024]{2,1,0:T(8,128)} %get-tuple-element.3) | copy-start | bytes 2359300
  79.3 40.5 %copy-start.7 = (f32[1,192,1024]{2,1,0:T(8,128)S(1)}, f32[1,192,1024]{2,1,0:T(8,128)}, u32[]{:S(2)}) copy-start(f32[1,192,1024]{2,1,0:T(8,128)} %get-tuple-element.10) | copy-start | bytes 2359300
  82.3 30.7 %collective-permute-start.6 = (f32[2,192,1024]{2,1,0:T(8,128)}, f32[2,192,1024]{2,1,0:T(8,128)}, u32[]{:S(2)}, u32[]{:S(2)}) collective-permute-start(f32[2,192,1024]{2,1,0:T(8,128)} %maximum_select_fusion.5), channel_id=1, source_target_pairs={{0,2},{16,18},{1,3},{17,19}} | collective-permute-start | bytes 4718600 | tf_op jit(solution)/shard_map/ppermute | solution.py:94
  97.6 21.1 %collective-permute-start.2 = (f32[2,192,1024]{2,1,0:T(8,128)}, f32[2,192,1024]{2,1,0:T(8,128)S(1)}, u32[]{:S(2)}, u32[]{:S(2)}) collective-permute-start(f32[2,192,1024]{2,1,0:T(8,128)} %maximum_select_fusion.3), channel_id=1, source_target_pairs={{0,6},{16,22},{1,7},{17,23}} | collective-permute-start | bytes 4718600 | tf_op jit(solution)/shard_map/ppermute | solution.py:94
  118.7 1.1 copy-start.10
  123.2 3.2 collective-permute-start.7
  139.3 3.8 copy-start.1
  139.3 3.8 copy-start.11
  149.6 10.7 %slice-start = ((s8[6160384]{0:T(1024)(128)(4,1)}), s8[4194304]{0:T(1024)(128)(4,1)S(1)}, s32[]{:S(2)}) async-start(s8[6160384]{0:T(1024)(128)(4,1)} %bitcast.61), calls=%async_computation.2 | async-start | bytes 8388608
  149.6 13.2 %slice-start.7 = ((s8[6160384]{0:T(1024)(128)(4,1)}), s8[4194304]{0:T(1024)(128)(4,1)S(1)}, s32[]{:S(2)}) async-start(s8[6160384]{0:T(1024)(128)(4,1)} %bitcast.65), calls=%async_computation.9 | async-start | bytes 8388608
  152.5 7.8 %slice-start.1 = ((s8[6160384]{0:T(1024)(128)(4,1)}), s8[1966080]{0:T(1024)(128)(4,1)S(1)}, s32[]{:S(2)}) async-start(s8[6160384]{0:T(1024)(128)(4,1)} %bitcast.61), calls=%async_computation.3 | async-start | bytes 3932160
  152.6 10.2 %slice-start.8 = ((s8[6160384]{0:T(1024)(128)(4,1)}), s8[1966080]{0:T(1024)(128)(4,1)S(1)}, s32[]{:S(2)}) async-start(s8[6160384]{0:T(1024)(128)(4,1)} %bitcast.65), calls=%async_computation.10 | async-start | bytes 3932160
  152.6 96.3 %collective-permute-start.10 = (f32[1056,1024]{1,0:T(8,128)S(1)}, f32[1056,1024]{1,0:T(8,128)S(1)}, u32[]{:S(2)}, u32[]{:S(2)}) collective-permute-start(f32[1056,1024]{1,0:T(8,128)S(1)} %slice.149), channel_id=1, source_target_pairs={{0,1},{1,0},{2,3},{3,2},{4,5},{5,4},{6,7},{7,6},{8,9},{9,8},{10,11... | collective-permute-start | bytes 12976136 | tf_op jit(solution)/shard_map/ppermute | solution.py:271
  159.4 182.2 %collective-permute-start.12 = (f32[1056,1024]{1,0:T(8,128)}, f32[1056,1024]{1,0:T(8,128)S(1)}, u32[]{:S(2)}, u32[]{:S(2)}) collective-permute-start(f32[1056,1024]{1,0:T(8,128)} %slice.153), channel_id=1, source_target_pairs={{0,1},{1,0},{2,3},{3,2},{4,5},{5,4},{6,7},{7,6},{8,9},{9,8},{10,11... | collective-permute-start | bytes 12976136 | tf_op jit(solution)/shard_map/ppermute | solution.py:271
  161.7 219.3 %collective-permute-start.9 = (f32[448,1024]{1,0:T(8,128)}, f32[448,1024]{1,0:T(8,128)}, u32[]{:S(2)}, u32[]{:S(2)}) collective-permute-start(f32[448,1024]{1,0:T(8,128)} %slice.148), channel_id=1, source_target_pairs={{0,1},{1,0},{2,3},{3,2},{4,5},{5,4},{6,7},{7,6},{8,9},{9,8},{10,11... | collective-permute-start | bytes 5505032 | tf_op jit(solution)/shard_map/ppermute | solution.py:272
  163.0 256.8 %collective-permute-start.11 = (f32[448,1024]{1,0:T(8,128)S(1)}, f32[448,1024]{1,0:T(8,128)}, u32[]{:S(2)}, u32[]{:S(2)}) collective-permute-start(f32[448,1024]{1,0:T(8,128)S(1)} %slice.152), channel_id=1, source_target_pairs={{0,1},{1,0},{2,3},{3,2},{4,5},{5,4},{6,7},{7,6},{8,9},{9,8},{10,11... | collective-permute-start | bytes 5505032 | tf_op jit(solution)/shard_map/ppermute | solution.py:272
  164.1 3.2 copy-start.12
  248.9 2.2 copy-start.3
  248.9 174.9 %slice-start.9 = ((s8[6160384]{0:T(1024)(128)(4,1)}), s8[4194304]{0:T(1024)(128)(4,1)S(1)}, s32[]{:S(2)}) async-start(s8[6160384]{0:T(1024)(128)(4,1)} %bitcast.67), calls=%async_computation.11 | async-start | bytes 8388608
  341.6 3.6 copy-start.4
  341.6 39.4 %slice-start.5 = ((f32[1504,1024]{1,0:T(8,128)}), f32[32,1024]{1,0:T(8,128)S(1)}, s32[]{:S(2)}) async-start(f32[1504,1024]{1,0:T(8,128)} %param.7), calls=%async_computation.7 | async-start | bytes 262144 | tf_op jit(solution)/shard_map/slice | solution.py:303
  341.6 39.4 %slice-start.14 = ((f32[1056,1024]{1,0:T(8,128)}), f32[32,1024]{1,0:T(8,128)S(1)}, s32[]{:S(2)}) async-start(f32[1056,1024]{1,0:T(8,128)} %copy-done.3), calls=%async_computation.16 | async-start | bytes 262144 | tf_op jit(solution)/shard_map/slice | solution.py:303
  341.6 82.2 %slice-start.10 = ((s8[6160384]{0:T(1024)(128)(4,1)}), s8[1966080]{0:T(1024)(128)(4,1)S(1)}, s32[]{:S(2)}) async-start(s8[6160384]{0:T(1024)(128)(4,1)} %bitcast.67), calls=%async_computation.12 | async-start | bytes 3932160
  345.2 74.6 %slice-start.12 = ((f32[1504,1024]{1,0:T(8,128)}), f32[32,1024]{1,0:T(8,128)S(1)}, s32[]{:S(2)}) async-start(f32[1504,1024]{1,0:T(8,128)} %param.6), calls=%async_computation.14 | async-start | bytes 262144 | tf_op jit(solution)/shard_map/slice | solution.py:303
  345.2 78.7 %slice-start.13 = ((f32[1504,1024]{1,0:T(8,128)}), f32[1472,1024]{1,0:T(8,128)S(1)}, s32[]{:S(2)}) async-start(f32[1504,1024]{1,0:T(8,128)} %param.6), calls=%async_computation.15 | async-start | bytes 12058624 | tf_op jit(solution)/shard_map/slice | solution.py:297
  419.7 13.8 %slice-start.2 = ((s8[6160384]{0:T(1024)(128)(4,1)}), s8[4194304]{0:T(1024)(128)(4,1)S(1)}, s32[]{:S(2)}) async-start(s8[6160384]{0:T(1024)(128)(4,1)} %bitcast.63), calls=%async_computation.4 | async-start | bytes 8388608
  423.8 9.7 %slice-start.3 = ((s8[6160384]{0:T(1024)(128)(4,1)}), s8[1966080]{0:T(1024)(128)(4,1)S(1)}, s32[]{:S(2)}) async-start(s8[6160384]{0:T(1024)(128)(4,1)} %bitcast.63), calls=%async_computation.5 | async-start | bytes 3932160
  423.9 9.7 %slice-start.6 = ((f32[1504,1024]{1,0:T(8,128)}), f32[1472,1024]{1,0:T(8,128)S(1)}, s32[]{:S(2)}) async-start(f32[1504,1024]{1,0:T(8,128)} %param.7), calls=%async_computation.8 | async-start | bytes 12058624 | tf_op jit(solution)/shard_map/slice | solution.py:297
  423.9 10.9 %slice-start.15 = ((f32[1056,1024]{1,0:T(8,128)}), f32[1024,1024]{1,0:T(8,128)S(1)}, s32[]{:S(2)}) async-start(f32[1056,1024]{1,0:T(8,128)} %copy-done.3), calls=%async_computation.17 | async-start | bytes 8388608 | tf_op jit(solution)/shard_map/slice | solution.py:297
  434.8 8.3 %copy-start.2 = (f32[16,2,32,1024]{3,2,1,0:T(8,128)S(1)}, f32[16,2,32,1024]{3,2,1,0:T(8,128)}, u32[]{:S(2)}) copy-start(f32[16,2,32,1024]{3,2,1,0:T(8,128)} %get-tuple-element.17) | copy-start | bytes 12582916
  443.1 14.2 %copy-start.5 = (f32[1024,1024]{0,1:T(8,128)S(1)}, f32[1024,1024]{0,1:T(8,128)}, u32[]{:S(2)}) copy-start(f32[1024,1024]{0,1:T(8,128)} %copy.10) | copy-start | bytes 12582916
  551.6 1.6 copy-start
Sparse Core Ops, SparseCore 0:
  16.5 57.1 all-gather.4
  149.7 104.1 all-gather.6
